TPU v7x, 32 devices: a whole 2x2x4 slice. The times are simulated.
32 devices in a mesh: fsdp: 16 (over z, y, x), rep: 2 (over core).
Axes of the slice: x: 2, y: 2, z: 4, core: 2. Of those that a mesh axis runs over, the one named last changes fastest.
Arguments:
- params: float32 [1536, 3584], P(('fsdp', 'rep')), may hold values from -6 to 6
- grads: bfloat16 [1536, 3584], P(('fsdp', 'rep')), may hold values from -6 to 6
- moments: bfloat16 [3, 1536, 3584], P(None, ('fsdp', 'rep')), may hold values from -6 to 6
- row_acc: float32 [1536], P(('fsdp', 'rep')), may hold values from 0.05 to 1
- lengths: int32 [32], replicated, may hold values from 1 to 384, 1536 in all
- tensor_order: int32 [32], replicated, may hold values from 0 to 31, each once
- col_acc: float32 [32, 3584], P('fsdp'), may hold values from 0.05 to 1
- hidden_state: float32 [32, 512], P('fsdp'), may hold values from -1 to 1
- cell_state: float32 [32, 512], P('fsdp'), may hold values from -4 to 4
- lstm_in: bfloat16 [10, 2048], replicated, may hold values from -2 to 2
- lstm_rec: bfloat16 [512, 2048], replicated, may hold values from -0.25 to 0.25
- lstm_bias: float32 [2048], replicated, may hold values from -3 to 3
- hyper_first: bfloat16 [512, 256], replicated, may hold values from -0.25 to 0.25
- hyper_rest: bfloat16 [512, 128], replicated, may hold values from -0.25 to 0.25
Outputs:
- update: float32 [1536, 3584], P(('fsdp', 'rep'))
- row_new: float32 [1536], P(('fsdp', 'rep'))
- col_new: float32 [32, 3584], P('fsdp')
- hidden_new: float32 [32, 512], P('fsdp')
- cell_new: float32 [32, 512], P('fsdp')
Inputs may be any that keep to these rules, and one draw needn't show every extreme that they name: `lengths`: they sum to 1536; the largest is 384. `tensor_order`: owner slot i belongs to fsdp index i // 2; each tensor appears once.
All inputs are finite; a program needn't handle non-finite values.
Results may differ from a plain program's by a relative error of at most 0.019.
Values may be sent and summed in bfloat16 or wider, within the bound.
A program may use at most 64 MiB of HBM per device.

v0:
```python
import math
import jax
import jax.numpy as jnp
from jax import lax
from jax.sharding import PartitionSpec as P

EPSILON = 1e-06
DECAY_RATE = 0.9


def owner_step(
    col_sums,
    tensor_stats,
    row_lengths,
    col_acc,
    hidden_state,
    cell_state,
    lstm_in,
    lstm_rec,
    lstm_bias,
    hyper_first,
    hyper_rest,
):
    col_width = col_acc.shape[1]
    col_new = DECAY_RATE * col_acc + (1.0 - DECAY_RATE) * col_sums / row_lengths[:, None]
    tensor_means = tensor_stats / (row_lengths * col_width)[:, None]
    log_means = jnp.log(tensor_means[:, :5] + EPSILON)
    corr_first = tensor_means[:, 5] / jnp.sqrt(tensor_means[:, 0] * tensor_means[:, 1] + EPSILON)
    corr_second = tensor_means[:, 6] / jnp.sqrt(tensor_means[:, 0] * tensor_means[:, 3] + EPSILON)
    corr_third = tensor_means[:, 7] / jnp.sqrt(tensor_means[:, 1] * tensor_means[:, 3] + EPSILON)
    col_mean = jnp.mean(col_new, axis=1)
    col_square = jnp.mean(col_new * col_new, axis=1)
    spread = jnp.log(col_square / (col_mean * col_mean))
    extra = jnp.stack(
        [corr_first, corr_second, corr_third, jnp.log(col_mean + EPSILON), spread], axis=1
    )
    features = jnp.concatenate([log_means, extra], axis=1).astype(jnp.bfloat16)
    gate_sum = jnp.dot(features, lstm_in, preferred_element_type=jnp.float32)
    gate_sum = (
        gate_sum
        + jnp.dot(hidden_state.astype(jnp.bfloat16), lstm_rec, preferred_element_type=jnp.float32)
        + lstm_bias
    )
    hid_width = hidden_state.shape[1]
    gate_in = gate_sum[:, :hid_width]
    gate_forget = gate_sum[:, hid_width : 2 * hid_width]
    gate_cand = gate_sum[:, 2 * hid_width : 3 * hid_width]
    gate_out = gate_sum[:, 3 * hid_width :]
    cell_new = jax.nn.sigmoid(gate_forget) * cell_state + jax.nn.sigmoid(gate_in) * jnp.tanh(
        gate_cand
    )
    hidden_new = jax.nn.sigmoid(gate_out) * jnp.tanh(cell_new)
    hidden_bf = hidden_new.astype(jnp.bfloat16)
    gen_first = jnp.dot(hidden_bf, hyper_first, preferred_element_type=jnp.float32).astype(
        jnp.bfloat16
    )
    gen_rest = jnp.dot(hidden_bf, hyper_rest, preferred_element_type=jnp.float32).astype(
        jnp.bfloat16
    )
    tensor_scales = jnp.stack(
        [
            jnp.sqrt(tensor_means[:, 0] + EPSILON),
            jnp.sqrt(tensor_means[:, 1] + EPSILON),
            jnp.sqrt(tensor_means[:, 4] + EPSILON),
            col_mean,
        ],
        axis=1,
    )
    return (col_new, hidden_new, cell_new, gen_first, gen_rest, tensor_scales)


def param_block(
    param_rows, grad_rows, moment_rows, row_var, col_rows, first_rows, rest_rows, scale_rows
):
    block_rows = param_rows.shape[0]
    grad_f = grad_rows.astype(jnp.float32)
    mom_f = moment_rows.astype(jnp.float32)
    v_factored = row_var[:, None] * col_rows / scale_rows[:, 3:4]
    inv_rms = lax.rsqrt(v_factored + EPSILON)
    grad_norm = grad_f * inv_rms
    mom_norm = mom_f[0] * inv_rms
    inputs = jnp.stack(
        [
            grad_norm,
            mom_norm,
            mom_f[1] * inv_rms,
            mom_f[2] * inv_rms,
            grad_f / scale_rows[:, 0:1],
            mom_f[0] / scale_rows[:, 1:2],
            param_rows / scale_rows[:, 2:3],
            grad_norm * mom_norm,
        ],
        axis=1,
    ).astype(jnp.bfloat16)
    hm_width = rest_rows.shape[1] // 4
    w_first = first_rows.reshape(block_rows, 8, hm_width)
    bias_first = rest_rows[:, :hm_width].astype(jnp.float32)
    w_second = rest_rows[:, hm_width:].reshape(block_rows, hm_width, 3)
    hidden_units = (
        jnp.einsum("bfc,bfh->bhc", inputs, w_first, preferred_element_type=jnp.float32)
        + bias_first[:, :, None]
    )
    hidden_units = jax.nn.relu(hidden_units).astype(jnp.bfloat16)
    mlp_out = jnp.einsum("bhc,bho->boc", hidden_units, w_second, preferred_element_type=jnp.float32)
    return mlp_out[:, 0] * jnp.exp(jnp.tanh(mlp_out[:, 1])) * jax.nn.sigmoid(mlp_out[:, 2])


def on_device(
    params,
    grads,
    moments,
    row_acc,
    lengths,
    tensor_order,
    col_acc,
    hidden_state,
    cell_state,
    lstm_in,
    lstm_rec,
    lstm_bias,
    hyper_first,
    hyper_rest,
):
    row_count = params.shape[0]
    tensor_count = lengths.shape[0]
    own_count = col_acc.shape[0]
    first_row = (lax.axis_index("fsdp") * lax.axis_size("rep") + lax.axis_index("rep")) * row_count
    tensor_ends = jnp.cumsum(lengths)
    global_rows = first_row + lax.iota(jnp.int32, row_count)
    seg_ids = jnp.sum((global_rows[:, None] >= tensor_ends[None, :]).astype(jnp.int32), axis=1)
    row_pick = (seg_ids[:, None] == tensor_order[None, :]).astype(jnp.float32)
    slot_match = tensor_order[:, None] == lax.iota(jnp.int32, tensor_count)[None, :]
    row_lengths = jnp.sum(jnp.where(slot_match, lengths[None, :], 0), axis=1).astype(jnp.float32)
    grad_f = grads.astype(jnp.float32)
    grad_sq = grad_f * grad_f
    row_new = DECAY_RATE * row_acc + (1.0 - DECAY_RATE) * jnp.mean(grad_sq, axis=1)
    mom_zero = moments[0].astype(jnp.float32)
    mom_one = moments[1].astype(jnp.float32)
    mom_two = moments[2].astype(jnp.float32)
    per_row = jnp.stack(
        [
            jnp.sum(grad_sq, axis=1),
            jnp.sum(mom_zero * mom_zero, axis=1),
            jnp.sum(mom_one * mom_one, axis=1),
            jnp.sum(mom_two * mom_two, axis=1),
            jnp.sum(params * params, axis=1),
            jnp.sum(grad_f * mom_zero, axis=1),
            jnp.sum(grad_f * mom_two, axis=1),
            jnp.sum(mom_zero * mom_two, axis=1),
        ],
        axis=1,
    )
    slot_stats = jnp.einsum("ri,rk->ik", row_pick, per_row, precision=lax.Precision.HIGHEST)
    slot_cols = jnp.einsum("ri,rc->ic", row_pick, grad_sq, precision=lax.Precision.HIGHEST)
    mine_start = lax.axis_index("fsdp") * own_count
    col_total, stats_total = lax.psum((slot_cols, slot_stats), ("fsdp", "rep"))
    col_prev, hidden_all, cell_all = (
        lax.all_gather(col_acc, "fsdp", axis=0, tiled=True),
        lax.all_gather(hidden_state, "fsdp", axis=0, tiled=True),
        lax.all_gather(cell_state, "fsdp", axis=0, tiled=True),
    )
    col_all, hidden_every, cell_every, first_all, rest_all, scale_all = owner_step(
        col_total,
        stats_total,
        row_lengths,
        col_prev,
        hidden_all,
        cell_all,
        lstm_in,
        lstm_rec,
        lstm_bias,
        hyper_first,
        hyper_rest,
    )
    col_new = lax.dynamic_slice_in_dim(col_all, mine_start, own_count, 0)
    hidden_new = lax.dynamic_slice_in_dim(hidden_every, mine_start, own_count, 0)
    cell_new = lax.dynamic_slice_in_dim(cell_every, mine_start, own_count, 0)
    col_rows = jnp.dot(row_pick, col_all, precision=lax.Precision.HIGHEST)
    scale_rows = jnp.dot(row_pick, scale_all, precision=lax.Precision.HIGHEST)
    pick_bf = row_pick.astype(jnp.bfloat16)
    first_rows = jnp.dot(pick_bf, first_all, preferred_element_type=jnp.float32).astype(
        jnp.bfloat16
    )
    rest_rows = jnp.dot(pick_bf, rest_all, preferred_element_type=jnp.float32).astype(jnp.bfloat16)
    block_rows = math.gcd(row_count, 16)
    block_count = row_count // block_rows

    def one_block(index):
        start = index * block_rows
        return param_block(
            lax.dynamic_slice_in_dim(params, start, block_rows, 0),
            lax.dynamic_slice_in_dim(grads, start, block_rows, 0),
            lax.dynamic_slice_in_dim(moments, start, block_rows, 1),
            lax.dynamic_slice_in_dim(row_new, start, block_rows, 0),
            lax.dynamic_slice_in_dim(col_rows, start, block_rows, 0),
            lax.dynamic_slice_in_dim(first_rows, start, block_rows, 0),
            lax.dynamic_slice_in_dim(rest_rows, start, block_rows, 0),
            lax.dynamic_slice_in_dim(scale_rows, start, block_rows, 0),
        )

    update = lax.map(one_block, lax.iota(jnp.int32, block_count)).reshape(params.shape)
    return (update, row_new, col_new, hidden_new, cell_new)


def solution(mesh):
    placed = (
        P(("fsdp", "rep"), None),
        P(("fsdp", "rep"), None),
        P(None, ("fsdp", "rep"), None),
        P(("fsdp", "rep")),
        P(),
        P(),
        P("fsdp", None),
        P("fsdp", None),
        P("fsdp", None),
        P(),
        P(),
        P(),
        P(),
        P(),
    )
    return jax.shard_map(
        on_device,
        mesh=mesh,
        in_specs=placed,
        out_specs=(
            P(("fsdp", "rep"), None),
            P(("fsdp", "rep")),
            P("fsdp", None),
            P("fsdp", None),
            P("fsdp", None),
        ),
        check_vma=False,
    )
```

profile of v0, /device:TPU:0, one launch (start us, length us, event | category | flops | bytes accessed | tf_op | source)
XLA Modules:
  0.0 245.1 jit_solution(586881530292995540)
XLA Ops:
  7.3 0.9 copy.76
  8.4 2.3 fusion.25
  10.7 0.9 select_reduce_fusion
  11.6 1.2 multiply_reduce_fusion.1
  12.7 1.7 fusion.30
  14.4 1.2 multiply_reduce_fusion
  16.5 42.0 %psum.14 = f32[32,8]{0,1:T(8,128)S(1)} all-reduce(f32[32,8]{0,1:T(8,128)S(1)} %fusion.50), channel_id=1, replica_groups=mesh['fsdp'=16,'rep'=2] {'fsdp','rep'}, use_global_device_ids=true, to_apply=%region_12.13 | all-reduce | flops 256 | bytes 2048 | tf_op jit(solution)/shard_map/psum | solution.py:156
  59.1 39.8 %all-gather.1 = bf16[16,2,512]{2,1,0:T(2,128)(2,1)S(1)} all-gather(bf16[1,2,512]{2,1,0:T(2,128)(2,1)S(1)} %bitcast_convert_fusion), channel_id=1, replica_groups=mesh['fsdp'=16,'rep'=2] {'fsdp'}, dimensions={0}, use_global_device_ids=true | all-gather | bytes 34816 | tf_op jit(solution)/shard_map/all_gather | solution.py:159
  98.9 38.4 %all-gather = f32[16,2,3584]{2,1,0:T(2,128)S(1)} all-gather(f32[1,2,3584]{2,1,0:T(2,128)S(1)} %bitcast.121), channel_id=1, replica_groups=mesh['fsdp'=16,'rep'=2] {'fsdp'}, dimensions={0}, use_global_device_ids=true | all-gather | bytes 487424 | tf_op jit(solution)/shard_map/all_gather | solution.py:158
  138.1 37.8 %all-gather.2 = f32[16,2,512]{2,1,0:T(2,128)S(1)} all-gather(f32[1,2,512]{2,1,0:T(2,128)S(1)} %bitcast.122), channel_id=1, replica_groups=mesh['fsdp'=16,'rep'=2] {'fsdp'}, dimensions={0}, use_global_device_ids=true | all-gather | bytes 69632 | tf_op jit(solution)/shard_map/all_gather | solution.py:160
  176.9 1.3 multiply_reduce_fusion.2
  178.2 2.0 fusion.47
  182.7 0.9 convolution_convert_fusion
  183.8 54.4 %while.10 = (s32[]{:T(128)}, f32[3,16,3584]{2,1,0:T(8,128)}, s32[3]{0:T(128)S(1)}, bf16[48,128]{1,0:T(8,128)(2,1)S(1)}, bf16[48,256]{1,0:T(8,128)(2,1)}, /*index...) while((s32[]{:T(128)}, f32[3,16,3584]{2,1,0:T(8,128)}, ...), condition=%wide.region_16.17_spmd, body=%wide.region_15.16_spmd.sunk | while | flops 47481352 | bytes 11314883 | solution.py:201
  187.0 1.0 dynamic-slice_convert_fusion.4
  188.4 1.3 fusion.104
  190.6 0.9 copy.132
  191.5 0.9 copy.133
  192.4 5.5 %stack.83 = bf16[16,8,3584]{2,1,0:T(8,128)(2,1)} concatenate(bf16[16,1,3584]{2,1,0:T(2,128)(2,1)S(1)} %copy.127, bf16[16,1,3584]{2,1,0:T(2,128)(2,1)S(1)} %copy.128, bf16[16,1,3584]{2,1,0:T(2,128)(2,1)S(1)} %copy.129, bf16[16,1,3584]{2,1,0:T(2,128)(2,1)S(1)} %copy.130, bf16[16,1,3584]{2,1,0:T(2,128)(2,1)S(1)} %copy.131, bf16[16,1,3584]{2,1,0:T(2,128)(2,1)S(1)} %fusion.105, ...), dimensions={1} | concatenate | bytes 1835008 | tf_op jit(solution)/shard_map/while/body/eval_jaxpr/stack | solution.py:82
  197.9 2.8 %fusion.106 = f32[16,3,3584]{2,1,0:T(4,128)S(1)} fusion(bf16[16,32,3]{1,2,0:T(4,128)(2,1)S(1)} %copy.126, bf16[16,8,32]{2,1,0:T(8,128)(2,1)S(1)} %reshape.216, bf16[16,8,3584]{2,1,0:T(8,128)(2,1)} %stack.83, f32[16,32]{1,0:T(8,128)S(1)} %dynamic-slice_convert_fusion.5), kind=kOutput, calls=%fused_computation.1.clone.1 | convolution fusion | flops 45875200 | bytes 1618944 | tf_op jit(solution)/shard_map/while/body/eval_jaxpr/bhc,bho->boc/dot_general | solution.py:104
  205.2 1.0 dynamic-slice_convert_fusion.4
  206.5 1.3 fusion.104
  208.8 0.9 copy.132
  209.7 0.9 copy.133
  210.5 5.5 %stack.83 = bf16[16,8,3584]{2,1,0:T(8,128)(2,1)} concatenate(bf16[16,1,3584]{2,1,0:T(2,128)(2,1)S(1)} %copy.127, bf16[16,1,3584]{2,1,0:T(2,128)(2,1)S(1)} %copy.128, bf16[16,1,3584]{2,1,0:T(2,128)(2,1)S(1)} %copy.129, bf16[16,1,3584]{2,1,0:T(2,128)(2,1)S(1)} %copy.130, bf16[16,1,3584]{2,1,0:T(2,128)(2,1)S(1)} %copy.131, bf16[16,1,3584]{2,1,0:T(2,128)(2,1)S(1)} %fusion.105, ...), dimensions={1} | concatenate | bytes 1835008 | tf_op jit(solution)/shard_map/while/body/eval_jaxpr/stack | solution.py:82
  216.0 2.8 %fusion.106 = f32[16,3,3584]{2,1,0:T(4,128)S(1)} fusion(bf16[16,32,3]{1,2,0:T(4,128)(2,1)S(1)} %copy.126, bf16[16,8,32]{2,1,0:T(8,128)(2,1)S(1)} %reshape.216, bf16[16,8,3584]{2,1,0:T(8,128)(2,1)} %stack.83, f32[16,32]{1,0:T(8,128)S(1)} %dynamic-slice_convert_fusion.5), kind=kOutput, calls=%fused_computation.1.clone.1 | convolution fusion | flops 45875200 | bytes 1618944 | tf_op jit(solution)/shard_map/while/body/eval_jaxpr/bhc,bho->boc/dot_general | solution.py:104
  223.3 1.0 dynamic-slice_convert_fusion.4
  224.7 1.3 fusion.104
  226.9 0.9 copy.132
  227.8 0.9 copy.133
  228.7 5.5 %stack.83 = bf16[16,8,3584]{2,1,0:T(8,128)(2,1)} concatenate(bf16[16,1,3584]{2,1,0:T(2,128)(2,1)S(1)} %copy.127, bf16[16,1,3584]{2,1,0:T(2,128)(2,1)S(1)} %copy.128, bf16[16,1,3584]{2,1,0:T(2,128)(2,1)S(1)} %copy.129, bf16[16,1,3584]{2,1,0:T(2,128)(2,1)S(1)} %copy.130, bf16[16,1,3584]{2,1,0:T(2,128)(2,1)S(1)} %copy.131, bf16[16,1,3584]{2,1,0:T(2,128)(2,1)S(1)} %fusion.105, ...), dimensions={1} | concatenate | bytes 1835008 | tf_op jit(solution)/shard_map/while/body/eval_jaxpr/stack | solution.py:82
  234.2 2.8 %fusion.106 = f32[16,3,3584]{2,1,0:T(4,128)S(1)} fusion(bf16[16,32,3]{1,2,0:T(4,128)(2,1)S(1)} %copy.126, bf16[16,8,32]{2,1,0:T(8,128)(2,1)S(1)} %reshape.216, bf16[16,8,3584]{2,1,0:T(8,128)(2,1)} %stack.83, f32[16,32]{1,0:T(8,128)S(1)} %dynamic-slice_convert_fusion.5), kind=kOutput, calls=%fused_computation.1.clone.1 | convolution fusion | flops 45875200 | bytes 1618944 | tf_op jit(solution)/shard_map/while/body/eval_jaxpr/bhc,bho->boc/dot_general | solution.py:104
  (116 shorter events, 21.2 us)
Async XLA Ops:
  7.2 130.4 %copy-start = (bf16[512,2048]{1,0:T(8,128)(2,1)S(1)}, bf16[512,2048]{1,0:T(8,128)(2,1)}, u32[]{:S(2)}) copy-start(bf16[512,2048]{1,0:T(8,128)(2,1)} %param.26) | copy-start | bytes 6291460
  7.2 9.1 %copy-start.6 = (s32[32]{0:T(128)S(1)}, s32[32]{0:T(128)}, u32[]{:S(2)}) copy-start(s32[32]{0:T(128)} %param.21) | copy-start | bytes 388
  7.2 8.5 %copy-start.10 = (f32[2,512]{1,0:T(2,128)S(1)}, f32[2,512]{1,0:T(2,128)}, u32[]{:S(2)}) copy-start(f32[2,512]{1,0:T(2,128)} %param.23) | copy-start | bytes 12292
  7.2 8.5 %copy-start.11 = (f32[48]{0:T(128)S(1)}, f32[48]{0:T(128)}, u32[]{:S(2)}) copy-start(f32[48]{0:T(128)} %param.19) | copy-start | bytes 580
  7.2 91.7 %copy-start.4 = (f32[2,3584]{1,0:T(2,128)S(1)}, f32[2,3584]{1,0:T(2,128)}, u32[]{:S(2)}) copy-start(f32[2,3584]{1,0:T(2,128)} %param.22) | copy-start | bytes 86020
  7.2 169.6 %all-reduce.2.cloned.1.call-start = ((), (), s32[]{:S(2)}) async-start(), calls=%async_computation | async-start | bytes 917504 | tf_op jit(solution)/shard_map/psum | solution.py:156
  8.4 7.9 %copy-start.7 = (s32[48]{0:T(128)}, s32[48]{0:T(128)S(1)}, u32[]{:S(2)}) copy-start(s32[48]{0:T(128)S(1)} %convert_reduce_fusion) | copy-start | bytes 580
  15.7 122.4 %copy-start.9 = (f32[2,512]{1,0:T(2,128)S(1)}, f32[2,512]{1,0:T(2,128)}, u32[]{:S(2)}) copy-start(f32[2,512]{1,0:T(2,128)} %param.24) | copy-start | bytes 12292
  138.0 43.5 %copy-start.3 = (bf16[10,2048]{1,0:T(8,128)(2,1)S(1)}, bf16[10,2048]{1,0:T(8,128)(2,1)}, u32[]{:S(2)}) copy-start(bf16[10,2048]{1,0:T(8,128)(2,1)} %param.25) | copy-start | bytes 122884
  138.0 43.5 %copy-start.5 = (f32[2048]{0:T(1024)S(1)}, f32[2048]{0:T(1024)}, u32[]{:S(2)}) copy-start(f32[2048]{0:T(1024)} %param.27) | copy-start | bytes 24580
  176.5 6.0 %copy-start.2 = (bf16[512,128]{1,0:T(8,128)(2,1)S(1)}, bf16[512,128]{1,0:T(8,128)(2,1)}, u32[]{:S(2)}) copy-start(bf16[512,128]{1,0:T(8,128)(2,1)} %param.29) | copy-start | bytes 393220
  176.8 5.7 %copy-start.8 = (s32[48]{0:T(128)S(1)}, s32[48]{0:T(128)}, u32[]{:S(2)}) copy-start(s32[48]{0:T(128)} %copy-done.7) | copy-start | bytes 580
  176.8 5.9 %copy-start.1 = (bf16[512,256]{1,0:T(8,128)(2,1)S(1)}, bf16[512,256]{1,0:T(8,128)(2,1)}, u32[]{:S(2)}) copy-start(bf16[512,256]{1,0:T(8,128)(2,1)} %param.28) | copy-start | bytes 786436
Sparse Core Ops, SparseCore 0:
  13.3 130.1 all-reduce.1
where the time goes:
time: 247 us; the launch traced here: 245 us
  blocking collectives  158 us (64%)
  local copies, waits for them, and re-layouts  36.7 us (15%)
  other arithmetic  19 us (8%)
  matrix products  14.8 us (6%)
  between operations  14.3 us (6%)
    psum x1, blocking collectives, on_device(): col_total, stats_total = lax.psum((slot_cols, slot_stats), ('fsdp', 'rep'))  42 us
    all_gather x1, blocking collectives, on_device(): lax.all_gather(hidden_state, 'fsdp', axis=0, tiled=True)  39.8 us
    all_gather x1, blocking collectives, on_device(): lax.all_gather(col_acc, 'fsdp', axis=0, tiled=True)  38.4 us
    all_gather x1, blocking collectives, on_device(): lax.all_gather(cell_state, 'fsdp', axis=0, tiled=True)  37.8 us
    another operation x24, local copies, waits for them, and re-layouts, param_block(): jnp.stack([grad_norm, mom_norm, mom_f[1] * inv_rms, mom_f[2] * inv_rms, g...  24.4 us
    dot_general x3, matrix products, param_block(): jnp.einsum('bhc,bho->boc', hidden_units, w_second, preferred_element_type...  8.4 us
  transfers between devices with their start and end apart: 1, of which 0 were waited for; matrix products, arithmetic and copies ran while one was open for 3% of the time, Pallas kernels for 0%

commit v1 on v0

--- a/solution.py
+++ b/solution.py
@@ -6,6 +6,12 @@
 
 EPSILON = 1e-06
 DECAY_RATE = 0.9
+
+
+def close_inputs(row_axis, comm_axis, content):
+    for j in (row_axis, comm_axis):
+        content = lax.psum(content, axis_name=j)
+    return content
 
 
 def owner_step(
@@ -153,7 +159,7 @@
     slot_stats = jnp.einsum("ri,rk->ik", row_pick, per_row, precision=lax.Precision.HIGHEST)
     slot_cols = jnp.einsum("ri,rc->ic", row_pick, grad_sq, precision=lax.Precision.HIGHEST)
     mine_start = lax.axis_index("fsdp") * own_count
-    col_total, stats_total = lax.psum((slot_cols, slot_stats), ("fsdp", "rep"))
+    col_total, stats_total = close_inputs("fsdp", "rep", (slot_cols, slot_stats))
     col_prev, hidden_all, cell_all = (
         lax.all_gather(col_acc, "fsdp", axis=0, tiled=True),
         lax.all_gather(hidden_state, "fsdp", axis=0, tiled=True),

time: 247 us -> 256 us (1.036)
  waiting for transfers between devices: 0.04 us -> 15.9 us
  local copies, waits for them, and re-layouts: 36.7 us -> 32.5 us
    psum x1 -> x2, waiting for transfers between devices: 0.02 us -> 15.9 us  [close_inputs(): content = lax.psum(content, axis_name=j)]
    all_gather x1, blocking collectives: 39.8 us -> 35.7 us  [on_device(): lax.all_gather(hidden_state, 'fsdp', axis=0, tiled=True)]
    psum x1 -> x2, blocking collectives: 42 us -> 46 us  [close_inputs(): content = lax.psum(content, axis_name=j)]
  transfers between devices with their start and end apart: 1 -> 2, of which waited for: 0 -> 1; matrix products, arithmetic and copies ran while one was open for 3% -> 2% of each run, Pallas kernels for 0% -> 0%
where the time goes in v1:
time: 256 us; the launch traced here: 254 us
  blocking collectives  158 us (62%)
  local copies, waits for them, and re-layouts  32.5 us (13%)
  other arithmetic  17.3 us (7%)
  waiting for transfers between devices  15.9 us (6%)
  between operations  14.3 us (6%)
  matrix products  13.6 us (5%)
    psum x2, blocking collectives, close_inputs(): content = lax.psum(content, axis_name=j)  46 us
    all_gather x1, blocking collectives, on_device(): lax.all_gather(col_acc, 'fsdp', axis=0, tiled=True)  40.7 us
    all_gather x1, blocking collectives, on_device(): lax.all_gather(cell_state, 'fsdp', axis=0, tiled=True)  35.8 us
    all_gather x1, blocking collectives, on_device(): lax.all_gather(hidden_state, 'fsdp', axis=0, tiled=True)  35.7 us
    another operation x24, local copies, waits for them, and re-layouts, param_block(): jnp.stack([grad_norm, mom_norm, mom_f[1] * inv_rms, mom_f[2] * inv_rms, g...  24.4 us
    psum x2, waiting for transfers between devices, close_inputs(): content = lax.psum(content, axis_name=j)  15.9 us
    dot_general x3, matrix products, param_block(): jnp.einsum('bhc,bho->boc', hidden_units, w_second, preferred_element_type...  8.42 us
  transfers between devices with their start and end apart: 2, of which 1 were waited for; matrix products, arithmetic and copies ran while one was open for 2% of the time, Pallas kernels for 0%

profile of v1, /device:TPU:0, one launch (start us, length us, event | category | flops | bytes accessed | tf_op | source)
XLA Modules:
  0.0 254.1 jit_solution(17385882150223232363)
XLA Ops:
  7.3 0.9 copy.76
  8.4 2.3 fusion.25
  11.6 1.2 multiply_reduce_fusion.1
  12.8 1.7 fusion.30
  14.5 1.2 multiply_reduce_fusion
  16.0 43.5 %psum.28 = f32[32,8]{0,1:T(8,128)S(1)} all-reduce(f32[32,8]{0,1:T(8,128)S(1)} %fusion.50), channel_id=1, replica_groups=mesh['fsdp'=16,'rep'=2] {'fsdp'}, use_global_device_ids=true, to_apply=%region_13.14 | all-reduce | flops 256 | bytes 2048 | tf_op jit(solution)/shard_map/psum | solution.py:13
  59.5 2.5 psum.29
  62.0 35.8 %all-gather.2 = f32[16,2,512]{2,1,0:T(2,128)S(1)} all-gather(f32[1,2,512]{2,1,0:T(2,128)S(1)} %bitcast.122), channel_id=1, replica_groups=mesh['fsdp'=16,'rep'=2] {'fsdp'}, dimensions={0}, use_global_device_ids=true | all-gather | bytes 69632 | tf_op jit(solution)/shard_map/all_gather | solution.py:166
  97.8 40.7 %all-gather = f32[16,2,3584]{2,1,0:T(2,128)S(1)} all-gather(f32[1,2,3584]{2,1,0:T(2,128)S(1)} %bitcast.121), channel_id=1, replica_groups=mesh['fsdp'=16,'rep'=2] {'fsdp'}, dimensions={0}, use_global_device_ids=true | all-gather | bytes 487424 | tf_op jit(solution)/shard_map/all_gather | solution.py:164
  138.7 35.7 %all-gather.1 = bf16[16,2,512]{2,1,0:T(2,128)(2,1)S(1)} all-gather(bf16[1,2,512]{2,1,0:T(2,128)(2,1)S(1)} %bitcast_convert_fusion), channel_id=1, replica_groups=mesh['fsdp'=16,'rep'=2] {'fsdp'}, dimensions={0}, use_global_device_ids=true | all-gather | bytes 34816 | tf_op jit(solution)/shard_map/all_gather | solution.py:165
  175.4 15.8 %all-reduce.5.cloned.1.call-done = f32[32,3584]{1,0:T(8,128)} async-done(((f32[32,3584]{1,0:T(8,128)}), f32[32,3584]{1,0:T(8,128)}) %all-reduce.5.cloned.1.call-update) | async-done | bytes 458768 | tf_op jit(solution)/shard_map/psum | solution.py:13
  191.3 1.3 multiply_reduce_fusion.2
  192.6 1.4 fusion.47
  196.3 50.5 %while.10 = (s32[]{:T(128)}, f32[3,16,3584]{2,1,0:T(8,128)}, s32[3]{0:T(128)S(1)}, bf16[48,128]{1,0:T(8,128)(2,1)S(1)}, bf16[48,256]{1,0:T(8,128)(2,1)S(1)}, /*i...) while((s32[]{:T(128)}, f32[3,16,3584]{2,1,0:T(8,128)}, ...), condition=%wide.region_18.19_spmd, body=%wide.region_17.18_spmd.sunk | while | flops 47481352 | bytes 11511547 | solution.py:207
  198.2 1.0 dynamic-slice_convert_fusion.4
  199.5 1.3 fusion.104
  201.8 0.9 copy.132
  202.7 0.9 copy.133
  203.5 5.5 %stack.83 = bf16[16,8,3584]{2,1,0:T(8,128)(2,1)} concatenate(bf16[16,1,3584]{2,1,0:T(2,128)(2,1)S(1)} %copy.127, bf16[16,1,3584]{2,1,0:T(2,128)(2,1)S(1)} %copy.128, bf16[16,1,3584]{2,1,0:T(2,128)(2,1)S(1)} %copy.129, bf16[16,1,3584]{2,1,0:T(2,128)(2,1)S(1)} %copy.130, bf16[16,1,3584]{2,1,0:T(2,128)(2,1)S(1)} %copy.131, bf16[16,1,3584]{2,1,0:T(2,128)(2,1)S(1)} %fusion.105, ...), dimensions={1} | concatenate | bytes 1835008 | tf_op jit(solution)/shard_map/while/body/eval_jaxpr/stack | solution.py:88
  209.0 2.8 %fusion.106 = f32[16,3,3584]{2,1,0:T(4,128)S(1)} fusion(bf16[16,32,3]{1,2,0:T(4,128)(2,1)S(1)} %copy.126, bf16[16,8,32]{2,1,0:T(8,128)(2,1)S(1)} %reshape.216, bf16[16,8,3584]{2,1,0:T(8,128)(2,1)} %stack.83, f32[16,32]{1,0:T(8,128)S(1)} %dynamic-slice_convert_fusion.5), kind=kOutput, calls=%fused_computation.1.clone.1 | convolution fusion | flops 45875200 | bytes 1618944 | tf_op jit(solution)/shard_map/while/body/eval_jaxpr/bhc,bho->boc/dot_general | solution.py:110
  215.0 1.0 dynamic-slice_convert_fusion.4
  216.3 1.3 fusion.104
  218.6 0.9 copy.132
  219.5 0.9 copy.133
  220.3 5.5 %stack.83 = bf16[16,8,3584]{2,1,0:T(8,128)(2,1)} concatenate(bf16[16,1,3584]{2,1,0:T(2,128)(2,1)S(1)} %copy.127, bf16[16,1,3584]{2,1,0:T(2,128)(2,1)S(1)} %copy.128, bf16[16,1,3584]{2,1,0:T(2,128)(2,1)S(1)} %copy.129, bf16[16,1,3584]{2,1,0:T(2,128)(2,1)S(1)} %copy.130, bf16[16,1,3584]{2,1,0:T(2,128)(2,1)S(1)} %copy.131, bf16[16,1,3584]{2,1,0:T(2,128)(2,1)S(1)} %fusion.105, ...), dimensions={1} | concatenate | bytes 1835008 | tf_op jit(solution)/shard_map/while/body/eval_jaxpr/stack | solution.py:88
  225.8 2.8 %fusion.106 = f32[16,3,3584]{2,1,0:T(4,128)S(1)} fusion(bf16[16,32,3]{1,2,0:T(4,128)(2,1)S(1)} %copy.126, bf16[16,8,32]{2,1,0:T(8,128)(2,1)S(1)} %reshape.216, bf16[16,8,3584]{2,1,0:T(8,128)(2,1)} %stack.83, f32[16,32]{1,0:T(8,128)S(1)} %dynamic-slice_convert_fusion.5), kind=kOutput, calls=%fused_computation.1.clone.1 | convolution fusion | flops 45875200 | bytes 1618944 | tf_op jit(solution)/shard_map/while/body/eval_jaxpr/bhc,bho->boc/dot_general | solution.py:110
  231.8 1.0 dynamic-slice_convert_fusion.4
  233.2 1.3 fusion.104
  235.4 0.9 copy.132
  236.3 0.9 copy.133
  237.1 5.5 %stack.83 = bf16[16,8,3584]{2,1,0:T(8,128)(2,1)} concatenate(bf16[16,1,3584]{2,1,0:T(2,128)(2,1)S(1)} %copy.127, bf16[16,1,3584]{2,1,0:T(2,128)(2,1)S(1)} %copy.128, bf16[16,1,3584]{2,1,0:T(2,128)(2,1)S(1)} %copy.129, bf16[16,1,3584]{2,1,0:T(2,128)(2,1)S(1)} %copy.130, bf16[16,1,3584]{2,1,0:T(2,128)(2,1)S(1)} %copy.131, bf16[16,1,3584]{2,1,0:T(2,128)(2,1)S(1)} %fusion.105, ...), dimensions={1} | concatenate | bytes 1835008 | tf_op jit(solution)/shard_map/while/body/eval_jaxpr/stack | solution.py:88
  242.6 2.8 %fusion.106 = f32[16,3,3584]{2,1,0:T(4,128)S(1)} fusion(bf16[16,32,3]{1,2,0:T(4,128)(2,1)S(1)} %copy.126, bf16[16,8,32]{2,1,0:T(8,128)(2,1)S(1)} %reshape.216, bf16[16,8,3584]{2,1,0:T(8,128)(2,1)} %stack.83, f32[16,32]{1,0:T(8,128)S(1)} %dynamic-slice_convert_fusion.5), kind=kOutput, calls=%fused_computation.1.clone.1 | convolution fusion | flops 45875200 | bytes 1618944 | tf_op jit(solution)/shard_map/while/body/eval_jaxpr/bhc,bho->boc/dot_general | solution.py:110
  (130 shorter events, 16.6 us)
Async XLA Ops:
  7.2 167.8 %copy-start = (bf16[512,2048]{1,0:T(8,128)(2,1)S(1)}, bf16[512,2048]{1,0:T(8,128)(2,1)}, u32[]{:S(2)}) copy-start(bf16[512,2048]{1,0:T(8,128)(2,1)} %param.26) | copy-start | bytes 6291460
  7.2 8.6 %copy-start.8 = (s32[32]{0:T(128)S(1)}, s32[32]{0:T(128)}, u32[]{:S(2)}) copy-start(s32[32]{0:T(128)} %param.21) | copy-start | bytes 388
  7.2 8.6 %copy-start.10 = (f32[2,512]{1,0:T(2,128)S(1)}, f32[2,512]{1,0:T(2,128)}, u32[]{:S(2)}) copy-start(f32[2,512]{1,0:T(2,128)} %param.23) | copy-start | bytes 12292
  7.2 54.8 %copy-start.9 = (f32[2,512]{1,0:T(2,128)S(1)}, f32[2,512]{1,0:T(2,128)}, u32[]{:S(2)}) copy-start(f32[2,512]{1,0:T(2,128)} %param.24) | copy-start | bytes 12292
  7.2 90.6 %copy-start.6 = (f32[2,3584]{1,0:T(2,128)S(1)}, f32[2,3584]{1,0:T(2,128)}, u32[]{:S(2)}) copy-start(f32[2,3584]{1,0:T(2,128)} %param.22) | copy-start | bytes 86020
  7.2 167.6 %all-reduce.3.cloned.1.call-start = ((), (), s32[]{:S(2)}) async-start(), calls=%async_computation | async-start | bytes 917504 | tf_op jit(solution)/shard_map/psum | solution.py:13
  10.7 180.6 %all-reduce.5.cloned.1.call-start = ((), (), s32[]{:S(2)}) async-start(), calls=%async_computation.1 | async-start | bytes 917504 | tf_op jit(solution)/shard_map/psum | solution.py:13
  14.5 160.4 %copy-start.11 = (f32[48]{0:T(128)S(1)}, f32[48]{0:T(128)}, u32[]{:S(2)}) copy-start(f32[48]{0:T(128)} %param.19) | copy-start | bytes 580
  174.9 19.7 %copy-start.5 = (bf16[10,2048]{1,0:T(8,128)(2,1)S(1)}, bf16[10,2048]{1,0:T(8,128)(2,1)}, u32[]{:S(2)}) copy-start(bf16[10,2048]{1,0:T(8,128)(2,1)} %param.25) | copy-start | bytes 122884
  174.9 19.7 %copy-start.7 = (f32[2048]{0:T(1024)S(1)}, f32[2048]{0:T(1024)}, u32[]{:S(2)}) copy-start(f32[2048]{0:T(1024)} %param.27) | copy-start | bytes 24580
  175.4 20.1 %copy-start.4 = (bf16[512,128]{1,0:T(8,128)(2,1)S(1)}, bf16[512,128]{1,0:T(8,128)(2,1)}, u32[]{:S(2)}) copy-start(bf16[512,128]{1,0:T(8,128)(2,1)} %param.29) | copy-start | bytes 393220
  175.4 20.4 %copy-start.1 = (bf16[512,256]{1,0:T(8,128)(2,1)S(1)}, bf16[512,256]{1,0:T(8,128)(2,1)}, u32[]{:S(2)}) copy-start(bf16[512,256]{1,0:T(8,128)(2,1)} %param.28) | copy-start | bytes 786436
  196.3 4.6 %copy-start.2 = (bf16[48,256]{1,0:T(8,128)(2,1)}, bf16[48,256]{1,0:T(8,128)(2,1)S(1)}, u32[]{:S(2)}) copy-start(bf16[48,256]{1,0:T(8,128)(2,1)S(1)} %get-tuple-element.295) | copy-start | bytes 73732 | tf_op jit(solution)/shard_map/while
  209.0 4.1 %copy-start.3 = (bf16[48,256]{1,0:T(8,128)(2,1)S(1)}, bf16[48,256]{1,0:T(8,128)(2,1)}, u32[]{:S(2)}) copy-start(bf16[48,256]{1,0:T(8,128)(2,1)} %copy-done.2) | copy-start | bytes 73732 | tf_op jit(solution)/shard_map/while
  213.1 4.5 %copy-start.2 = (bf16[48,256]{1,0:T(8,128)(2,1)}, bf16[48,256]{1,0:T(8,128)(2,1)S(1)}, u32[]{:S(2)}) copy-start(bf16[48,256]{1,0:T(8,128)(2,1)S(1)} %get-tuple-element.295) | copy-start | bytes 73732 | tf_op jit(solution)/shard_map/while
  225.8 4.1 %copy-start.3 = (bf16[48,256]{1,0:T(8,128)(2,1)S(1)}, bf16[48,256]{1,0:T(8,128)(2,1)}, u32[]{:S(2)}) copy-start(bf16[48,256]{1,0:T(8,128)(2,1)} %copy-done.2) | copy-start | bytes 73732 | tf_op jit(solution)/shard_map/while
  229.9 4.5 %copy-start.2 = (bf16[48,256]{1,0:T(8,128)(2,1)}, bf16[48,256]{1,0:T(8,128)(2,1)S(1)}, u32[]{:S(2)}) copy-start(bf16[48,256]{1,0:T(8,128)(2,1)S(1)} %get-tuple-element.295) | copy-start | bytes 73732 | tf_op jit(solution)/shard_map/while
  242.6 4.1 %copy-start.3 = (bf16[48,256]{1,0:T(8,128)(2,1)S(1)}, bf16[48,256]{1,0:T(8,128)(2,1)}, u32[]{:S(2)}) copy-start(bf16[48,256]{1,0:T(8,128)(2,1)} %copy-done.2) | copy-start | bytes 73732 | tf_op jit(solution)/shard_map/while
  246.8 0.5 copy-start.12
Sparse Core Ops, SparseCore 0:
  13.2 111.7 all-reduce.2
  175.0 16.2 all-reduce.4
